TPU v7x, 32 devices: a whole 2x2x4 slice. The times are simulated.
32 devices in a mesh: segment: 8 (over z, x), dp: 4 (over y, core).
Axes of the slice: x: 2, y: 2, z: 4, core: 2. Of those that a mesh axis runs over, the one named last changes fastest.
Arguments:
- src_embed: bfloat16 [16, 128, 2048], P('dp', None, 'segment'), parts along dimension 0, may hold values from -6 to 6
- tgt_embed: bfloat16 [16, 128, 2048], P('dp', None, 'segment'), parts along dimension 0, may hold values from -6 to 6
- src_lengths: int32 [16], P('dp'), parts along dimension 0, may hold values from 32 to 128
- tgt_lengths: int32 [16], P('dp'), parts along dimension 0, may hold values from 32 to 128
- attn_in: bfloat16 [8, 2048, 3072], P('segment'), may hold values from -0.125 to 0.125
- attn_out: bfloat16 [8, 1024, 2048], P('segment'), may hold values from -0.375 to 0.375
- norm_gain: float32 [4, 2048], replicated, may hold values from 0.25 to 1.75
- final_gain: float32 [2048], replicated, may hold values from 0.25 to 1.75
Outputs:
- decoded: bfloat16 [16, 128, 2048], P('dp', None, 'segment'), parts along dimension 0
There are 4 independent parts, one for each index of `dp`. A program takes and returns all parts, laid end to end along the dimension named above; an argument that names none is the same for every part. Nothing has to cross between parts.
Inputs may be any that keep to these rules, and one draw needn't show every extreme that they name: `src_lengths`: keys at positions below a sequence's length are its real tokens. `tgt_lengths`: keys at positions below a sequence's length are its real tokens.
All inputs are finite; a program needn't handle non-finite values.
Results may differ from a plain program's by a relative error of at most 0.015.
Values may be sent and summed in bfloat16 or wider, within the bound.
A program may use at most 64 MiB of HBM per device.

v0:
```python
import jax
import jax.numpy as jnp
from jax import lax
from jax.sharding import PartitionSpec as P

HEAD = 64


epsilon = 1e-06
score_scale = 0.125


def partner(value, axis, distance):
    mask = 2**distance
    pairs = [(source, source ^ mask) for source in range(lax.axis_size(axis))]
    return lax.ppermute(value, axis, pairs)


def shifted(value, axis, by):
    length = lax.axis_size(axis)
    pairs = [(i, i + by) for i in range(length) if 0 <= i + by < length]
    return lax.ppermute(value, axis, pairs)


def rms_scale(values, gain_vector):
    return (
        values
        * lax.rsqrt(jnp.mean(values * values, axis=-1, keepdims=True) + epsilon)
        * gain_vector
    )


def attention(queries, key_rows, values, allowed):
    head_count = queries.shape[1] // HEAD
    shaped_q = queries.reshape(queries.shape[0], head_count, HEAD)
    shaped_k = key_rows.reshape(key_rows.shape[0], head_count, HEAD)
    shaped_v = values.reshape(values.shape[0], head_count, HEAD)
    scores = (
        jnp.einsum("qhd,khd->hqk", shaped_q, shaped_k, preferred_element_type=jnp.float32)
        * score_scale
    )
    scores = jnp.where(allowed[None], scores, -1000000000.0)
    weights = jax.nn.softmax(scores, axis=-1).astype(jnp.bfloat16)
    mixture = jnp.einsum("hqk,khd->qhd", weights, shaped_v, preferred_element_type=jnp.float32)
    return mixture.reshape(queries.shape[0], -1).astype(jnp.bfloat16)


def pick_row(array, row_slot):
    return lax.dynamic_index_in_dim(array, row_slot, 0, keepdims=False)


def place_row(array, row_slot, update, keep_flag):
    former = pick_row(array, row_slot)
    return lax.dynamic_update_index_in_dim(array, jnp.where(keep_flag, update, former), row_slot, 0)


def on_device(
    src_embed, tgt_embed, src_lengths, tgt_lengths, attn_in, attn_out, norm_gain, final_gain
):
    segments = lax.axis_size("segment")
    group_size = segments // 4
    bit_count = group_size.bit_length() - 1
    segment_index = lax.axis_index("segment")
    section = segment_index // group_size
    member = segment_index % group_size
    batches, seq_len, column_share = src_embed.shape
    full_width = column_share * segments
    destination = (jnp.arange(segments, dtype=jnp.int32) // group_size)[None, None, :, None]
    outgoing = jnp.where(
        destination == 0,
        src_embed[:, :, None, :],
        jnp.where(destination == 2, tgt_embed[:, :, None, :], jnp.zeros((), jnp.bfloat16)),
    )
    arrived = lax.all_to_all(outgoing, "segment", split_axis=2, concat_axis=2, tiled=True)
    embedded = arrived.reshape(batches, seq_len, full_width)
    in_weight = attn_in[0]
    out_weight = attn_out[0]
    head_cols = out_weight.shape[0]
    layer_gain = pick_row(norm_gain, section)
    positions = jnp.arange(seq_len, dtype=jnp.int32)
    causal = positions[None, :] <= positions[:, None]
    is_target = section == 3
    starts_chain = (section == 0) | (section == 2)

    def allowed_for(batch_slot):
        seq_length = jnp.where(
            is_target, pick_row(tgt_lengths, batch_slot), pick_row(src_lengths, batch_slot)
        )
        return (positions[None, :] < seq_length) & (causal | jnp.logical_not(is_target))

    def head_partial(current, memory, batch_slot):
        normed = rms_scale(current.astype(jnp.float32), layer_gain).astype(jnp.bfloat16)
        source = jnp.where(section == 2, memory, normed)
        queries = jnp.dot(
            normed, in_weight[:, :head_cols], preferred_element_type=jnp.float32
        ).astype(jnp.bfloat16)
        key_value = jnp.dot(
            source, in_weight[:, head_cols:], preferred_element_type=jnp.float32
        ).astype(jnp.bfloat16)
        mixture = attention(
            queries, key_value[:, :head_cols], key_value[:, head_cols:], allowed_for(batch_slot)
        )
        return jnp.dot(mixture, out_weight, preferred_element_type=jnp.float32)

    def combine_heads(current, partial_sum):
        summed = partial_sum
        for bit_index in range(bit_count):
            summed = summed + partner(summed, "segment", bit_index)
        return (current.astype(jnp.float32) + summed).astype(jnp.bfloat16)

    def final_norm(output):
        return rms_scale(output.astype(jnp.float32), final_gain).astype(jnp.bfloat16)

    zero_sum = jnp.zeros((seq_len, full_width), jnp.float32)

    def run_sublayer(step_index, received):
        slot_raw = step_index - section
        active = (slot_raw >= 0) & (slot_raw < batches)
        batch_slot = jnp.clip(slot_raw, 0, batches - 1)
        current = jnp.where(starts_chain, pick_row(embedded, batch_slot), received)
        partial_sum = lax.cond(
            active,
            lambda value_in, memory_in: head_partial(value_in, memory_in, batch_slot),
            lambda value_in, memory_in: zero_sum,
            current,
            received,
        )
        output = combine_heads(current, partial_sum)
        return (output, batch_slot, active)

    empty_rows = jnp.zeros((seq_len, full_width), jnp.bfloat16)
    collected = jnp.zeros((batches, seq_len, full_width), jnp.bfloat16)

    def relay_step(step_index, state_tuple):
        received, outputs = state_tuple
        output, batch_slot, active = run_sublayer(step_index, received)
        outputs = place_row(outputs, batch_slot, output, active & (section == 3))
        leaving = jnp.where(section == 1, final_norm(output), output)
        forwarded = shifted(leaving, "segment", group_size)
        return (forwarded, outputs)

    state_tuple = lax.fori_loop(0, batches + 3, relay_step, (empty_rows, collected))
    outputs = state_tuple[1]
    decoded_cols = lax.dynamic_slice_in_dim(outputs, segment_index * column_share, column_share, 2)
    for distance in range(1, 4):
        chosen = lax.dynamic_slice_in_dim(
            outputs, ((3 - distance) * group_size + member) * column_share, column_share, 2
        )
        incoming = shifted(chosen, "segment", -distance * group_size)
        decoded_cols = jnp.where(section == 3 - distance, incoming, decoded_cols)
    return decoded_cols


def solution(mesh):
    in_specs = (
        P("dp", None, "segment"),
        P("dp", None, "segment"),
        P("dp"),
        P("dp"),
        P("segment", None, None),
        P("segment", None, None),
        P(),
        P(),
    )
    out_specs = P("dp", None, "segment")
    return jax.shard_map(
        on_device, mesh=mesh, in_specs=in_specs, out_specs=out_specs, check_vma=False
    )
```

profile of v0, /device:TPU:0, one launch (start us, length us, event | category | flops | bytes accessed | tf_op | source)
XLA Modules:
  0.0 422.1 jit_solution(14281037983660344813)
XLA Ops:
  0.0 2.7 select_select_fusion
  2.7 7.3 %all-to-all-start = ((bf16[4,128,8,256]{3,1,0,2:T(8,128)(2,1)}), bf16[4,128,8,256]{3,1,0,2:T(8,128)(2,1)S(1)}, u32[]{:S(2)}, u32[]{:S(2)}) async-start(bf16[4,128,8,256]{3,1,0,2:T(8,128)(2,1)} %select_select_fusion), calls=%async_computation | async-start | bytes 4194304 | tf_op jit(solution)/shard_map/all_to_all | solution.py:74
  10.0 48.2 %all-to-all-done = bf16[4,128,8,256]{3,1,0,2:T(8,128)(2,1)S(1)} async-done(((bf16[4,128,8,256]{3,1,0,2:T(8,128)(2,1)}), bf16[4,128,8,256]{3,1,0,2:T(8,128)(2,1)S(1)}, u32[]{:S(2)}, u32[]{:S(2)}) %all-to-all-start) | async-done | bytes 2097184 | tf_op jit(solution)/shard_map/all_to_all | solution.py:74
  58.2 2.4 copy.25
  60.5 1.6 broadcast_in_dim.85
  62.2 326.8 %while.18 = (s32[]{:T(128)}, bf16[128,2048]{1,0:T(8,128)(2,1)S(1)}, bf16[4,128,2048]{2,1,0:T(8,128)(2,1)}, pred[]{:T(512)}, pred[]{:T(512)}, /*index=5*/s32[]{:T...) while((s32[]{:T(128)}, bf16[128,2048]{1,0:T(8,128)(2,1)S(1)}, ...), condition=%wide.region_7.8_spmd.clone, body=%wide.region_0.7_spmd.clone.sunk | while | flops 2257898240 | bytes 44399368 | solution.py:142
  63.6 15.2 %conditional.3 = (f32[128,2048]{1,0:T(8,128)S(1)}) conditional(s32[]{:T(128)} %convert_element_type.120, () %tuple.56, (s32[]{:T(128)}, bf16[128,2048]{1,0:T(8,128)(2,1)S(1)}, f32[2048]{0:T(1024)S(1)}, bf16[128,2048]{1,0:T(8,128)(2,1)S(1)}, bf16[2048,3072]{1,0:T(8,128)(2,1)}, /*index=5*/s32[]{:T(128)}, s32[4]{0:T(128)S(1)}, s32[4]{0:T(128)S(1)}, ...), branch_computations={%region_1.1_spmd, %region_2.5_spmd} | conditional | flops 2254227968 | bytes 27479392 | solution.py:121
  66.4 4.7 %fusion.9 = bf16[128,2048]{1,0:T(8,128)(2,1)S(1)} fusion(bf16[2048,3072]{1,0:T(8,128)(2,1)} %get-tuple-element.369, bf16[128,2048]{1,0:T(8,128)(2,1)S(1)} %get-tuple-element.366, pred[]{:T(512)S(6)} %eq.42, bf16[128,2048]{1,0:T(8,128)(2,1)S(1)} %get-tuple-element.367, f32[2048]{0:T(1024)S(1)} %get-tuple-element.368, f32[128]{0:T(128)S(1)} %add_rsqrt_fusion), kind=kOutput, calls=%fused_computation.7 | convolution fusion | flops 1075314688 | bytes 9970177 | tf_op jit(solution)/shard_map/while/body/eval_jaxpr/cond/branch_1_fun/dot_general | solution.py:97
  71.3 3.0 fusion.15
  75.9 2.9 fusion.35
  78.9 1.5 collective-permute-start
  81.5 21.3 %collective-permute-done = f32[128,2048]{1,0:T(8,128)S(1)} collective-permute-done((f32[128,2048]{1,0:T(8,128)S(1)}, f32[128,2048]{1,0:T(8,128)S(1)}, u32[]{:S(2)}, u32[]{:S(2)}) %collective-permute-start) | collective-permute-done | bytes 1048608 | tf_op jit(solution)/shard_map/while/body/eval_jaxpr/ppermute | solution.py:16
  105.7 9.5 %collective-permute-done.1 = bf16[128,2048]{1,0:T(8,128)(2,1)S(1)} collective-permute-done((bf16[128,2048]{1,0:T(8,128)(2,1)S(1)}, bf16[128,2048]{1,0:T(8,128)(2,1)S(1)}, u32[]{:S(2)}, u32[]{:S(2)}) %collective-permute-start.1) | collective-permute-done | bytes 524320 | tf_op jit(solution)/shard_map/while/body/eval_jaxpr/ppermute | solution.py:22
  116.7 15.2 %conditional.3 = (f32[128,2048]{1,0:T(8,128)S(1)}) conditional(s32[]{:T(128)} %convert_element_type.120, () %tuple.56, (s32[]{:T(128)}, bf16[128,2048]{1,0:T(8,128)(2,1)S(1)}, f32[2048]{0:T(1024)S(1)}, bf16[128,2048]{1,0:T(8,128)(2,1)S(1)}, bf16[2048,3072]{1,0:T(8,128)(2,1)}, /*index=5*/s32[]{:T(128)}, s32[4]{0:T(128)S(1)}, s32[4]{0:T(128)S(1)}, ...), branch_computations={%region_1.1_spmd, %region_2.5_spmd} | conditional | flops 2254227968 | bytes 27479392 | solution.py:121
  119.5 4.7 %fusion.9 = bf16[128,2048]{1,0:T(8,128)(2,1)S(1)} fusion(bf16[2048,3072]{1,0:T(8,128)(2,1)} %get-tuple-element.369, bf16[128,2048]{1,0:T(8,128)(2,1)S(1)} %get-tuple-element.366, pred[]{:T(512)S(6)} %eq.42, bf16[128,2048]{1,0:T(8,128)(2,1)S(1)} %get-tuple-element.367, f32[2048]{0:T(1024)S(1)} %get-tuple-element.368, f32[128]{0:T(128)S(1)} %add_rsqrt_fusion), kind=kOutput, calls=%fused_computation.7 | convolution fusion | flops 1075314688 | bytes 9970177 | tf_op jit(solution)/shard_map/while/body/eval_jaxpr/cond/branch_1_fun/dot_general | solution.py:97
  124.4 2.9 fusion.15
  129.0 2.9 fusion.35
  131.9 2.1 collective-permute-start
  135.1 19.9 %collective-permute-done = f32[128,2048]{1,0:T(8,128)S(1)} collective-permute-done((f32[128,2048]{1,0:T(8,128)S(1)}, f32[128,2048]{1,0:T(8,128)S(1)}, u32[]{:S(2)}, u32[]{:S(2)}) %collective-permute-start) | collective-permute-done | bytes 1048608 | tf_op jit(solution)/shard_map/while/body/eval_jaxpr/ppermute | solution.py:16
  156.6 4.4 %collective-permute-start.1 = (bf16[128,2048]{1,0:T(8,128)(2,1)S(1)}, bf16[128,2048]{1,0:T(8,128)(2,1)S(1)}, u32[]{:S(2)}, u32[]{:S(2)}) collective-permute-start(bf16[128,2048]{1,0:T(8,128)(2,1)S(1)} %fusion.47), channel_id=1, source_target_pairs={{0,8},{4,12},{8,16},{12,20},{16,24},{20,28},{1,9},{5,13},{9,17},{1... | collective-permute-start | bytes 1572872 | tf_op jit(solution)/shard_map/while/body/eval_jaxpr/ppermute | solution.py:22
  161.0 8.4 %collective-permute-done.1 = bf16[128,2048]{1,0:T(8,128)(2,1)S(1)} collective-permute-done((bf16[128,2048]{1,0:T(8,128)(2,1)S(1)}, bf16[128,2048]{1,0:T(8,128)(2,1)S(1)}, u32[]{:S(2)}, u32[]{:S(2)}) %collective-permute-start.1) | collective-permute-done | bytes 524320 | tf_op jit(solution)/shard_map/while/body/eval_jaxpr/ppermute | solution.py:22
  170.8 15.2 %conditional.3 = (f32[128,2048]{1,0:T(8,128)S(1)}) conditional(s32[]{:T(128)} %convert_element_type.120, () %tuple.56, (s32[]{:T(128)}, bf16[128,2048]{1,0:T(8,128)(2,1)S(1)}, f32[2048]{0:T(1024)S(1)}, bf16[128,2048]{1,0:T(8,128)(2,1)S(1)}, bf16[2048,3072]{1,0:T(8,128)(2,1)}, /*index=5*/s32[]{:T(128)}, s32[4]{0:T(128)S(1)}, s32[4]{0:T(128)S(1)}, ...), branch_computations={%region_1.1_spmd, %region_2.5_spmd} | conditional | flops 2254227968 | bytes 27479392 | solution.py:121
  173.6 4.7 %fusion.9 = bf16[128,2048]{1,0:T(8,128)(2,1)S(1)} fusion(bf16[2048,3072]{1,0:T(8,128)(2,1)} %get-tuple-element.369, bf16[128,2048]{1,0:T(8,128)(2,1)S(1)} %get-tuple-element.366, pred[]{:T(512)S(6)} %eq.42, bf16[128,2048]{1,0:T(8,128)(2,1)S(1)} %get-tuple-element.367, f32[2048]{0:T(1024)S(1)} %get-tuple-element.368, f32[128]{0:T(128)S(1)} %add_rsqrt_fusion), kind=kOutput, calls=%fused_computation.7 | convolution fusion | flops 1075314688 | bytes 9970177 | tf_op jit(solution)/shard_map/while/body/eval_jaxpr/cond/branch_1_fun/dot_general | solution.py:97
  178.5 3.0 fusion.15
  183.1 2.9 fusion.35
  186.0 1.5 collective-permute-start
  188.6 18.7 %collective-permute-done = f32[128,2048]{1,0:T(8,128)S(1)} collective-permute-done((f32[128,2048]{1,0:T(8,128)S(1)}, f32[128,2048]{1,0:T(8,128)S(1)}, u32[]{:S(2)}, u32[]{:S(2)}) %collective-permute-start) | collective-permute-done | bytes 1048608 | tf_op jit(solution)/shard_map/while/body/eval_jaxpr/ppermute | solution.py:16
  208.9 4.4 %collective-permute-start.1 = (bf16[128,2048]{1,0:T(8,128)(2,1)S(1)}, bf16[128,2048]{1,0:T(8,128)(2,1)S(1)}, u32[]{:S(2)}, u32[]{:S(2)}) collective-permute-start(bf16[128,2048]{1,0:T(8,128)(2,1)S(1)} %fusion.47), channel_id=1, source_target_pairs={{0,8},{4,12},{8,16},{12,20},{16,24},{20,28},{1,9},{5,13},{9,17},{1... | collective-permute-start | bytes 1572872 | tf_op jit(solution)/shard_map/while/body/eval_jaxpr/ppermute | solution.py:22
  213.4 6.7 %collective-permute-done.1 = bf16[128,2048]{1,0:T(8,128)(2,1)S(1)} collective-permute-done((bf16[128,2048]{1,0:T(8,128)(2,1)S(1)}, bf16[128,2048]{1,0:T(8,128)(2,1)S(1)}, u32[]{:S(2)}, u32[]{:S(2)}) %collective-permute-start.1) | collective-permute-done | bytes 524320 | tf_op jit(solution)/shard_map/while/body/eval_jaxpr/ppermute | solution.py:22
  221.5 15.2 %conditional.3 = (f32[128,2048]{1,0:T(8,128)S(1)}) conditional(s32[]{:T(128)} %convert_element_type.120, () %tuple.56, (s32[]{:T(128)}, bf16[128,2048]{1,0:T(8,128)(2,1)S(1)}, f32[2048]{0:T(1024)S(1)}, bf16[128,2048]{1,0:T(8,128)(2,1)S(1)}, bf16[2048,3072]{1,0:T(8,128)(2,1)}, /*index=5*/s32[]{:T(128)}, s32[4]{0:T(128)S(1)}, s32[4]{0:T(128)S(1)}, ...), branch_computations={%region_1.1_spmd, %region_2.5_spmd} | conditional | flops 2254227968 | bytes 27479392 | solution.py:121
  224.3 4.7 %fusion.9 = bf16[128,2048]{1,0:T(8,128)(2,1)S(1)} fusion(bf16[2048,3072]{1,0:T(8,128)(2,1)} %get-tuple-element.369, bf16[128,2048]{1,0:T(8,128)(2,1)S(1)} %get-tuple-element.366, pred[]{:T(512)S(6)} %eq.42, bf16[128,2048]{1,0:T(8,128)(2,1)S(1)} %get-tuple-element.367, f32[2048]{0:T(1024)S(1)} %get-tuple-element.368, f32[128]{0:T(128)S(1)} %add_rsqrt_fusion), kind=kOutput, calls=%fused_computation.7 | convolution fusion | flops 1075314688 | bytes 9970177 | tf_op jit(solution)/shard_map/while/body/eval_jaxpr/cond/branch_1_fun/dot_general | solution.py:97
  229.2 3.0 fusion.15
  233.8 2.9 fusion.35
  239.0 17.3 %collective-permute-done = f32[128,2048]{1,0:T(8,128)S(1)} collective-permute-done((f32[128,2048]{1,0:T(8,128)S(1)}, f32[128,2048]{1,0:T(8,128)S(1)}, u32[]{:S(2)}, u32[]{:S(2)}) %collective-permute-start) | collective-permute-done | bytes 1048608 | tf_op jit(solution)/shard_map/while/body/eval_jaxpr/ppermute | solution.py:16
  257.9 4.4 %collective-permute-start.1 = (bf16[128,2048]{1,0:T(8,128)(2,1)S(1)}, bf16[128,2048]{1,0:T(8,128)(2,1)S(1)}, u32[]{:S(2)}, u32[]{:S(2)}) collective-permute-start(bf16[128,2048]{1,0:T(8,128)(2,1)S(1)} %fusion.47), channel_id=1, source_target_pairs={{0,8},{4,12},{8,16},{12,20},{16,24},{20,28},{1,9},{5,13},{9,17},{1... | collective-permute-start | bytes 1572872 | tf_op jit(solution)/shard_map/while/body/eval_jaxpr/ppermute | solution.py:22
  262.3 6.6 %collective-permute-done.1 = bf16[128,2048]{1,0:T(8,128)(2,1)S(1)} collective-permute-done((bf16[128,2048]{1,0:T(8,128)(2,1)S(1)}, bf16[128,2048]{1,0:T(8,128)(2,1)S(1)}, u32[]{:S(2)}, u32[]{:S(2)}) %collective-permute-start.1) | collective-permute-done | bytes 524320 | tf_op jit(solution)/shard_map/while/body/eval_jaxpr/ppermute | solution.py:22
  272.3 16.2 %collective-permute-done = f32[128,2048]{1,0:T(8,128)S(1)} collective-permute-done((f32[128,2048]{1,0:T(8,128)S(1)}, f32[128,2048]{1,0:T(8,128)S(1)}, u32[]{:S(2)}, u32[]{:S(2)}) %collective-permute-start) | collective-permute-done | bytes 1048608 | tf_op jit(solution)/shard_map/while/body/eval_jaxpr/ppermute | solution.py:16
  290.0 19.2 %collective-permute-start.1 = (bf16[128,2048]{1,0:T(8,128)(2,1)S(1)}, bf16[128,2048]{1,0:T(8,128)(2,1)S(1)}, u32[]{:S(2)}, u32[]{:S(2)}) collective-permute-start(bf16[128,2048]{1,0:T(8,128)(2,1)S(1)} %fusion.47), channel_id=1, source_target_pairs={{0,8},{4,12},{8,16},{12,20},{16,24},{20,28},{1,9},{5,13},{9,17},{1... | collective-permute-start | bytes 1572872 | tf_op jit(solution)/shard_map/while/body/eval_jaxpr/ppermute | solution.py:22
  309.3 6.6 %collective-permute-done.1 = bf16[128,2048]{1,0:T(8,128)(2,1)S(1)} collective-permute-done((bf16[128,2048]{1,0:T(8,128)(2,1)S(1)}, bf16[128,2048]{1,0:T(8,128)(2,1)S(1)}, u32[]{:S(2)}, u32[]{:S(2)}) %collective-permute-start.1) | collective-permute-done | bytes 524320 | tf_op jit(solution)/shard_map/while/body/eval_jaxpr/ppermute | solution.py:22
  318.9 14.5 %collective-permute-done = f32[128,2048]{1,0:T(8,128)S(1)} collective-permute-done((f32[128,2048]{1,0:T(8,128)S(1)}, f32[128,2048]{1,0:T(8,128)S(1)}, u32[]{:S(2)}, u32[]{:S(2)}) %collective-permute-start) | collective-permute-done | bytes 1048608 | tf_op jit(solution)/shard_map/while/body/eval_jaxpr/ppermute | solution.py:16
  334.9 4.1 collective-permute-start.1
  339.1 6.6 %collective-permute-done.1 = bf16[128,2048]{1,0:T(8,128)(2,1)S(1)} collective-permute-done((bf16[128,2048]{1,0:T(8,128)(2,1)S(1)}, bf16[128,2048]{1,0:T(8,128)(2,1)S(1)}, u32[]{:S(2)}, u32[]{:S(2)}) %collective-permute-start.1) | collective-permute-done | bytes 524320 | tf_op jit(solution)/shard_map/while/body/eval_jaxpr/ppermute | solution.py:22
  348.7 13.4 %collective-permute-done = f32[128,2048]{1,0:T(8,128)S(1)} collective-permute-done((f32[128,2048]{1,0:T(8,128)S(1)}, f32[128,2048]{1,0:T(8,128)S(1)}, u32[]{:S(2)}, u32[]{:S(2)}) %collective-permute-start) | collective-permute-done | bytes 1048608 | tf_op jit(solution)/shard_map/while/body/eval_jaxpr/ppermute | solution.py:16
  363.7 18.7 %collective-permute-start.1 = (bf16[128,2048]{1,0:T(8,128)(2,1)S(1)}, bf16[128,2048]{1,0:T(8,128)(2,1)S(1)}, u32[]{:S(2)}, u32[]{:S(2)}) collective-permute-start(bf16[128,2048]{1,0:T(8,128)(2,1)S(1)} %fusion.47), channel_id=1, source_target_pairs={{0,8},{4,12},{8,16},{12,20},{16,24},{20,28},{1,9},{5,13},{9,17},{1... | collective-permute-start | bytes 1572872 | tf_op jit(solution)/shard_map/while/body/eval_jaxpr/ppermute | solution.py:22
  382.4 6.6 %collective-permute-done.1 = bf16[128,2048]{1,0:T(8,128)(2,1)S(1)} collective-permute-done((bf16[128,2048]{1,0:T(8,128)(2,1)S(1)}, bf16[128,2048]{1,0:T(8,128)(2,1)S(1)}, u32[]{:S(2)}, u32[]{:S(2)}) %collective-permute-start.1) | collective-permute-done | bytes 524320 | tf_op jit(solution)/shard_map/while/body/eval_jaxpr/ppermute | solution.py:22
  394.1 21.9 %collective-permute-done.2 = bf16[4,128,256]{2,1,0:T(8,128)(2,1)S(1)} collective-permute-done((bf16[4,128,256]{2,1,0:T(8,128)(2,1)S(1)}, bf16[4,128,256]{2,1,0:T(8,128)(2,1)S(1)}, u32[]{:S(2)}, u32[]{:S(2)}) %collective-permute-start.2) | collective-permute-done | bytes 262176 | tf_op jit(solution)/shard_map/ppermute | solution.py:22
  416.0 4.3 %collective-permute-done.3 = bf16[4,128,256]{2,1,0:T(8,128)(2,1)S(1)} collective-permute-done((bf16[4,128,256]{2,1,0:T(8,128)(2,1)S(1)}, bf16[4,128,256]{2,1,0:T(8,128)(2,1)S(1)}, u32[]{:S(2)}, u32[]{:S(2)}) %collective-permute-start.3) | collective-permute-done | bytes 262176 | tf_op jit(solution)/shard_map/ppermute | solution.py:22
  420.3 1.8 select_select_fusion.1
  (156 shorter events, 50.9 us)
Async XLA Ops:
  0.0 10.0 %copy-start = (f32[4,2048]{1,0:T(4,128)S(1)}, f32[4,2048]{1,0:T(4,128)}, u32[]{:S(2)}) copy-start(f32[4,2048]{1,0:T(4,128)} %param.18) | copy-start | bytes 98308
  2.7 55.5 %all-to-all-start = ((bf16[4,128,8,256]{3,1,0,2:T(8,128)(2,1)}), bf16[4,128,8,256]{3,1,0,2:T(8,128)(2,1)S(1)}, u32[]{:S(2)}, u32[]{:S(2)}) async-start(bf16[4,128,8,256]{3,1,0,2:T(8,128)(2,1)} %select_select_fusion), calls=%async_computation | async-start | bytes 4194304 | tf_op jit(solution)/shard_map/all_to_all | solution.py:74
  60.5 1.6 copy-start.1
  60.5 1.6 copy-start.2
  60.5 1.6 copy-start.3
  78.9 24.0 %collective-permute-start = (f32[128,2048]{1,0:T(8,128)S(1)}, f32[128,2048]{1,0:T(8,128)S(1)}, u32[]{:S(2)}, u32[]{:S(2)}) collective-permute-start(f32[128,2048]{1,0:T(8,128)S(1)} %get-tuple-element.623), channel_id=1, source_target_pairs={{0,4},{4,0},{8,12},{12,8},{16,20},{20,16},{24,28},{28,24},{1,5},{5... | collective-permute-start | bytes 3145736 | tf_op jit(solution)/shard_map/while/body/eval_jaxpr/ppermute | solution.py:16
  104.4 10.9 %collective-permute-start.1 = (bf16[128,2048]{1,0:T(8,128)(2,1)S(1)}, bf16[128,2048]{1,0:T(8,128)(2,1)S(1)}, u32[]{:S(2)}, u32[]{:S(2)}) collective-permute-start(bf16[128,2048]{1,0:T(8,128)(2,1)S(1)} %fusion.47), channel_id=1, source_target_pairs={{0,8},{4,12},{8,16},{12,20},{16,24},{20,28},{1,9},{5,13},{9,17},{1... | collective-permute-start | bytes 1572872 | tf_op jit(solution)/shard_map/while/body/eval_jaxpr/ppermute | solution.py:22
  131.9 23.1 %collective-permute-start = (f32[128,2048]{1,0:T(8,128)S(1)}, f32[128,2048]{1,0:T(8,128)S(1)}, u32[]{:S(2)}, u32[]{:S(2)}) collective-permute-start(f32[128,2048]{1,0:T(8,128)S(1)} %get-tuple-element.623), channel_id=1, source_target_pairs={{0,4},{4,0},{8,12},{12,8},{16,20},{20,16},{24,28},{28,24},{1,5},{5... | collective-permute-start | bytes 3145736 | tf_op jit(solution)/shard_map/while/body/eval_jaxpr/ppermute | solution.py:16
  156.6 12.8 %collective-permute-start.1 = (bf16[128,2048]{1,0:T(8,128)(2,1)S(1)}, bf16[128,2048]{1,0:T(8,128)(2,1)S(1)}, u32[]{:S(2)}, u32[]{:S(2)}) collective-permute-start(bf16[128,2048]{1,0:T(8,128)(2,1)S(1)} %fusion.47), channel_id=1, source_target_pairs={{0,8},{4,12},{8,16},{12,20},{16,24},{20,28},{1,9},{5,13},{9,17},{1... | collective-permute-start | bytes 1572872 | tf_op jit(solution)/shard_map/while/body/eval_jaxpr/ppermute | solution.py:22
  186.0 21.4 %collective-permute-start = (f32[128,2048]{1,0:T(8,128)S(1)}, f32[128,2048]{1,0:T(8,128)S(1)}, u32[]{:S(2)}, u32[]{:S(2)}) collective-permute-start(f32[128,2048]{1,0:T(8,128)S(1)} %get-tuple-element.623), channel_id=1, source_target_pairs={{0,4},{4,0},{8,12},{12,8},{16,20},{20,16},{24,28},{28,24},{1,5},{5... | collective-permute-start | bytes 3145736 | tf_op jit(solution)/shard_map/while/body/eval_jaxpr/ppermute | solution.py:16
  208.9 11.1 %collective-permute-start.1 = (bf16[128,2048]{1,0:T(8,128)(2,1)S(1)}, bf16[128,2048]{1,0:T(8,128)(2,1)S(1)}, u32[]{:S(2)}, u32[]{:S(2)}) collective-permute-start(bf16[128,2048]{1,0:T(8,128)(2,1)S(1)} %fusion.47), channel_id=1, source_target_pairs={{0,8},{4,12},{8,16},{12,20},{16,24},{20,28},{1,9},{5,13},{9,17},{1... | collective-permute-start | bytes 1572872 | tf_op jit(solution)/shard_map/while/body/eval_jaxpr/ppermute | solution.py:22
  236.7 19.6 %collective-permute-start = (f32[128,2048]{1,0:T(8,128)S(1)}, f32[128,2048]{1,0:T(8,128)S(1)}, u32[]{:S(2)}, u32[]{:S(2)}) collective-permute-start(f32[128,2048]{1,0:T(8,128)S(1)} %get-tuple-element.623), channel_id=1, source_target_pairs={{0,4},{4,0},{8,12},{12,8},{16,20},{20,16},{24,28},{28,24},{1,5},{5... | collective-permute-start | bytes 3145736 | tf_op jit(solution)/shard_map/while/body/eval_jaxpr/ppermute | solution.py:16
  257.9 11.1 %collective-permute-start.1 = (bf16[128,2048]{1,0:T(8,128)(2,1)S(1)}, bf16[128,2048]{1,0:T(8,128)(2,1)S(1)}, u32[]{:S(2)}, u32[]{:S(2)}) collective-permute-start(bf16[128,2048]{1,0:T(8,128)(2,1)S(1)} %fusion.47), channel_id=1, source_target_pairs={{0,8},{4,12},{8,16},{12,20},{16,24},{20,28},{1,9},{5,13},{9,17},{1... | collective-permute-start | bytes 1572872 | tf_op jit(solution)/shard_map/while/body/eval_jaxpr/ppermute | solution.py:22
  270.5 17.9 %collective-permute-start = (f32[128,2048]{1,0:T(8,128)S(1)}, f32[128,2048]{1,0:T(8,128)S(1)}, u32[]{:S(2)}, u32[]{:S(2)}) collective-permute-start(f32[128,2048]{1,0:T(8,128)S(1)} %get-tuple-element.623), channel_id=1, source_target_pairs={{0,4},{4,0},{8,12},{12,8},{16,20},{20,16},{24,28},{28,24},{1,5},{5... | collective-permute-start | bytes 3145736 | tf_op jit(solution)/shard_map/while/body/eval_jaxpr/ppermute | solution.py:16
  290.0 25.9 %collective-permute-start.1 = (bf16[128,2048]{1,0:T(8,128)(2,1)S(1)}, bf16[128,2048]{1,0:T(8,128)(2,1)S(1)}, u32[]{:S(2)}, u32[]{:S(2)}) collective-permute-start(bf16[128,2048]{1,0:T(8,128)(2,1)S(1)} %fusion.47), channel_id=1, source_target_pairs={{0,8},{4,12},{8,16},{12,20},{16,24},{20,28},{1,9},{5,13},{9,17},{1... | collective-permute-start | bytes 1572872 | tf_op jit(solution)/shard_map/while/body/eval_jaxpr/ppermute | solution.py:22
  317.5 15.9 %collective-permute-start = (f32[128,2048]{1,0:T(8,128)S(1)}, f32[128,2048]{1,0:T(8,128)S(1)}, u32[]{:S(2)}, u32[]{:S(2)}) collective-permute-start(f32[128,2048]{1,0:T(8,128)S(1)} %get-tuple-element.623), channel_id=1, source_target_pairs={{0,4},{4,0},{8,12},{12,8},{16,20},{20,16},{24,28},{28,24},{1,5},{5... | collective-permute-start | bytes 3145736 | tf_op jit(solution)/shard_map/while/body/eval_jaxpr/ppermute | solution.py:16
  334.9 10.8 %collective-permute-start.1 = (bf16[128,2048]{1,0:T(8,128)(2,1)S(1)}, bf16[128,2048]{1,0:T(8,128)(2,1)S(1)}, u32[]{:S(2)}, u32[]{:S(2)}) collective-permute-start(bf16[128,2048]{1,0:T(8,128)(2,1)S(1)} %fusion.47), channel_id=1, source_target_pairs={{0,8},{4,12},{8,16},{12,20},{16,24},{20,28},{1,9},{5,13},{9,17},{1... | collective-permute-start | bytes 1572872 | tf_op jit(solution)/shard_map/while/body/eval_jaxpr/ppermute | solution.py:22
  347.3 14.9 %collective-permute-start = (f32[128,2048]{1,0:T(8,128)S(1)}, f32[128,2048]{1,0:T(8,128)S(1)}, u32[]{:S(2)}, u32[]{:S(2)}) collective-permute-start(f32[128,2048]{1,0:T(8,128)S(1)} %get-tuple-element.623), channel_id=1, source_target_pairs={{0,4},{4,0},{8,12},{12,8},{16,20},{20,16},{24,28},{28,24},{1,5},{5... | collective-permute-start | bytes 3145736 | tf_op jit(solution)/shard_map/while/body/eval_jaxpr/ppermute | solution.py:16
  363.7 25.4 %collective-permute-start.1 = (bf16[128,2048]{1,0:T(8,128)(2,1)S(1)}, bf16[128,2048]{1,0:T(8,128)(2,1)S(1)}, u32[]{:S(2)}, u32[]{:S(2)}) collective-permute-start(bf16[128,2048]{1,0:T(8,128)(2,1)S(1)} %fusion.47), channel_id=1, source_target_pairs={{0,8},{4,12},{8,16},{12,20},{16,24},{20,28},{1,9},{5,13},{9,17},{1... | collective-permute-start | bytes 1572872 | tf_op jit(solution)/shard_map/while/body/eval_jaxpr/ppermute | solution.py:22
  390.2 25.8 %collective-permute-start.2 = (bf16[4,128,256]{2,1,0:T(8,128)(2,1)S(1)}, bf16[4,128,256]{2,1,0:T(8,128)(2,1)S(1)}, u32[]{:S(2)}, u32[]{:S(2)}) collective-permute-start(bf16[4,128,256]{2,1,0:T(8,128)(2,1)S(1)} %get-tuple-element.477), channel_id=1, source_target_pairs={{24,0},{28,4},{25,1},{29,5},{26,2},{30,6},{27,3},{31,7}} | collective-permute-start | bytes 786440 | tf_op jit(solution)/shard_map/ppermute | solution.py:22
  391.5 28.8 %collective-permute-start.3 = (bf16[4,128,256]{2,1,0:T(8,128)(2,1)S(1)}, bf16[4,128,256]{2,1,0:T(8,128)(2,1)S(1)}, u32[]{:S(2)}, u32[]{:S(2)}) collective-permute-start(bf16[4,128,256]{2,1,0:T(8,128)(2,1)S(1)} %get-tuple-element.476), channel_id=1, source_target_pairs={{16,0},{20,4},{24,8},{28,12},{17,1},{21,5},{25,9},{29,13},{18,2},{... | collective-permute-start | bytes 786440 | tf_op jit(solution)/shard_map/ppermute | solution.py:22
  392.8 27.5 %collective-permute-start.4 = (bf16[4,128,256]{2,1,0:T(8,128)(2,1)S(1)}, bf16[4,128,256]{2,1,0:T(8,128)(2,1)S(1)}, u32[]{:S(2)}, u32[]{:S(2)}) collective-permute-start(bf16[4,128,256]{2,1,0:T(8,128)(2,1)S(1)} %get-tuple-element.475), channel_id=1, source_target_pairs={{8,0},{12,4},{16,8},{20,12},{24,16},{28,20},{9,1},{13,5},{17,9},{2... | collective-permute-start | bytes 786440 | tf_op jit(solution)/shard_map/ppermute | solution.py:22
where the time goes:
time: 424 us; the launch traced here: 422 us
  waiting for transfers between devices  247 us (58%)
  starting transfers between devices  75.5 us (18%)
  matrix products  47.3 us (11%)
  local copies, waits for them, and re-layouts  29.2 us (7%)
  other arithmetic  16.9 us (4%)
  loops' own time  6.02 us (1%)
    ppermute x7, waiting for transfers between devices, partner(): return lax.ppermute(value, axis, pairs)  121 us
    ppermute x10, waiting for transfers between devices, shifted(): return lax.ppermute(value, axis, pairs)  77.4 us
    ppermute x10, starting transfers between devices, shifted(): return lax.ppermute(value, axis, pairs)  60.5 us
    all_to_all x1, waiting for transfers between devices, on_device(): lax.all_to_all(outgoing, 'segment', split_axis=2, concat_axis=2, tiled=True)  48.2 us
    dynamic_slice x30, local copies, waits for them, and re-layouts, pick_row(): return lax.dynamic_index_in_dim(array, row_slot, 0, keepdims=False)  21.5 us
    dot_general x4, matrix products, head_partial(): jnp.dot(source, in_weight[:, head_cols:], preferred_element_type=jnp.floa...  18.8 us
    dot_general x4, matrix products, head_partial(): jnp.dot(normed, in_weight[:, :head_cols], preferred_element_type=jnp.floa...  11.8 us
    dot_general x4, matrix products, head_partial(): return jnp.dot(mixture, out_weight, preferred_element_type=jnp.float32)  11.7 us
  transfers between devices with their start and end apart: 18, of which 17 were waited for; matrix products, arithmetic and copies ran while one was open for 2% of the time, Pallas kernels for 0%

commit v1 on v0

v1 whole, which is shorter than its diff:
```python
import functools

import jax
import jax.numpy as jnp
from jax import lax
from jax.experimental import pallas as pl
from jax.experimental.pallas import tpu as pltpu
from jax.sharding import PartitionSpec as P

HEAD = 64
LAYERS = 4
MESH = pl.DeviceIdType.MESH
epsilon = 1e-06
score_scale = 0.125


def kernel(
    segs,
    src_len,
    tgt_len,
    src,
    tgt,
    w_in,
    w_out,
    gains,
    final_gain,
    out,
    win,
    wout,
    act,
    nrm,
    qkv,
    mix,
    own,
    ps,
    pr,
    fw,
    w_sem,
    act_sem,
    in_send,
    p_send,
    p_recv,
    f_send,
    o_recv,
):
    group = segs // LAYERS
    batches, seq, cw = src.shape
    width = segs * cw
    hc = wout.shape[0]
    me = lax.axis_index("segment")
    section = me // group
    member = me % group
    is_cross = section == 2
    is_last = section == LAYERS - 1
    q_src = jnp.where(is_cross, 1, 0)

    win_copy = pltpu.make_async_copy(w_in, win, w_sem.at[0])
    wout_copy = pltpu.make_async_copy(w_out, wout, w_sem.at[1])
    win_copy.start()
    wout_copy.start()

    barrier = pltpu.get_barrier_semaphore()
    for step in range(1, segs):
        pl.semaphore_signal(
            barrier,
            inc=1,
            device_id={"segment": lax.rem(me + step, segs)},
            device_id_type=MESH,
        )
    pl.semaphore_wait(barrier, segs - 1)

    def remote(source, dest, send, recv, target):
        return pltpu.make_async_remote_copy(
            src_ref=source,
            dst_ref=dest,
            send_sem=send,
            recv_sem=recv,
            device_id={"segment": target},
            device_id_type=MESH,
        )

    def input_copy(kind, m, j):
        ref = src if kind == 0 else tgt
        target = 2 * kind * group + j
        return remote(
            ref.at[m],
            act.at[kind, m, me],
            in_send.at[kind, m, j],
            act_sem.at[kind, m, me],
            target,
        )

    def send_inputs(kind, m):
        ref = src if kind == 0 else tgt
        for j in range(group):
            target = 2 * kind * group + j

            @pl.when(me != target)
            def _():
                input_copy(kind, m, j).start()

            @pl.when(me == target)
            def _():
                pltpu.make_async_copy(
                    ref.at[m], act.at[kind, m, me], act_sem.at[kind, m, me]
                ).start()

    for m in range(batches):
        send_inputs(0, m)
    for m in range(batches):
        send_inputs(1, m)

    def act_wait(kind, m, c):
        pltpu.make_async_copy(
            act.at[kind, m, c], act.at[kind, m, c], act_sem.at[kind, m, c]
        ).wait()

    def normalize(kind, m, gain_row):
        total = jnp.zeros((seq, cw), jnp.float32)
        for c in range(segs):
            v = act[kind, m, c].astype(jnp.float32)
            total = total + v * v
        mean = jnp.sum(total, axis=-1, keepdims=True) * (1.0 / width)
        scale = lax.rsqrt(mean + epsilon)
        for c in range(segs):
            v = act[kind, m, c].astype(jnp.float32)
            g = gain_row(c)
            nrm[kind, :, c * cw : (c + 1) * cw] = (v * scale * g).astype(jnp.bfloat16)

    def key_gain(c):
        cols = slice(c * cw, (c + 1) * cw)
        picked = jnp.where(is_cross, final_gain[:, cols], gains[0:1, cols])
        for p in (1, 3):
            picked = jnp.where(section == p, gains[p : p + 1, cols], picked)
        return picked

    def query_gain(c):
        return gains[2:3, c * cw : (c + 1) * cw]

    def part_copy(m, c, g):
        target = section * group + lax.rem(member + g, group)
        return remote(
            ps.at[m, c],
            pr.at[m, g - 1, c],
            p_send.at[m, g - 1, c],
            p_recv.at[m, g - 1, c],
            target,
        )

    def part_needed(c, g):
        goal = lax.rem(member + g, group)
        return jnp.logical_or(section < LAYERS - 1, lax.rem(c, group) == goal)

    def keeps(c):
        return jnp.logical_or(section < LAYERS - 1, lax.rem(c, group) == member)

    def next_copy(m, c):
        return remote(
            fw.at[m, c], act.at[0, m, c], f_send.at[m, c], act_sem.at[0, m, c], me + group
        )

    def out_copy(m, c):
        return remote(fw.at[m, c], out.at[m], f_send.at[m, c], o_recv.at[m], c)

    tile = min(512, hc)
    kv_tiles = 2 * hc // tile
    q_tiles = hc // tile

    def batch_step(m, carry):
        @pl.when(is_cross)
        def _():
            for c in range(segs):
                act_wait(1, m, c)
            normalize(1, m, query_gain)

        for c in range(segs):
            act_wait(0, m, c)

        normalize(0, m, key_gain)

        @pl.when(m == 0)
        def _():
            win_copy.wait()

        def project(t, carry):
            kind = jnp.where(t < q_tiles, q_src, 0)
            cols = pl.ds(pl.multiple_of(t * tile, tile), tile)
            qkv[:, cols] = jnp.dot(
                nrm[kind], win[:, cols], preferred_element_type=jnp.float32
            ).astype(jnp.bfloat16)
            return carry

        lax.fori_loop(0, q_tiles + kv_tiles, project, 0)

        length = jnp.where(is_last, tgt_len[m], src_len[m])
        keys = lax.broadcasted_iota(jnp.int32, (2 * seq, seq), 1)
        rows = lax.broadcasted_iota(jnp.int32, (2 * seq, seq), 0)
        rows = jnp.where(rows >= seq, rows - seq, rows)
        bound = jnp.where(is_last, rows, seq)
        allowed = (keys < length) & (keys <= bound)
        lane = lax.broadcasted_iota(jnp.int32, (seq, 2 * HEAD), 1)
        low = lane < HEAD
        for h in range(hc // (2 * HEAD)):
            at = h * 2 * HEAD
            q2 = qkv[:, at : at + 2 * HEAD]
            k2 = qkv[:, hc + at : hc + at + 2 * HEAD]
            v2 = qkv[:, 2 * hc + at : 2 * hc + at + 2 * HEAD]
            zero = jnp.zeros_like(q2)
            both = jnp.concatenate(
                [jnp.where(low, q2, zero), jnp.where(low, zero, q2)], axis=0
            )
            scores = (
                lax.dot_general(
                    both,
                    k2,
                    (((1,), (1,)), ((), ())),
                    preferred_element_type=jnp.float32,
                )
                * score_scale
            )
            scores = jnp.where(allowed, scores, -1000000000.0)
            top = jnp.max(scores, axis=-1, keepdims=True)
            e = jnp.exp(scores - top)
            weights = (e / jnp.sum(e, axis=-1, keepdims=True)).astype(jnp.bfloat16)
            o = jnp.dot(weights, v2, preferred_element_type=jnp.float32)
            mix[:, at : at + 2 * HEAD] = jnp.where(low, o[:seq], o[seq:]).astype(
                jnp.bfloat16
            )

        @pl.when(m == 0)
        def _():
            wout_copy.wait()

        def emit(c, carry):
            cols = pl.ds(pl.multiple_of(c * cw, cw), cw)
            part = jnp.dot(mix[...], wout[:, cols], preferred_element_type=jnp.float32)
            own[c] = part
            ps[m, c] = part.astype(jnp.bfloat16)
            for g in range(1, group):

                @pl.when(part_needed(c, g))
                def _():
                    part_copy(m, c, g).start()

            return carry

        lax.fori_loop(0, segs, emit, 0)

        def combine(c, carry):
            @pl.when(keeps(c))
            def _():
                total = own[c] + act[q_src, m, c].astype(jnp.float32)
                for g in range(1, group):
                    part_copy(m, c, g).wait_recv()
                    total = total + pr[m, g - 1, c].astype(jnp.float32)
                fw[m, c] = total.astype(jnp.bfloat16)

                @pl.when(section < LAYERS - 1)
                def _():
                    next_copy(m, c).start()

                @pl.when(jnp.logical_and(is_last, me != c))
                def _():
                    out_copy(m, c).start()

                @pl.when(jnp.logical_and(is_last, me == c))
                def _():
                    pltpu.make_async_copy(fw.at[m, c], out.at[m], o_recv.at[m]).start()

            return carry

        lax.fori_loop(0, segs, combine, 0)
        return carry

    lax.fori_loop(0, batches, batch_step, 0)

    def finish(m, carry):
        for kind in range(2):
            for j in range(group):

                @pl.when(me != 2 * kind * group + j)
                def _():
                    input_copy(kind, m, j).wait_send()

        def drain(c, carry):
            for g in range(1, group):

                @pl.when(part_needed(c, g))
                def _():
                    part_copy(m, c, g).wait_send()

            @pl.when(section < LAYERS - 1)
            def _():
                next_copy(m, c).wait_send()

            @pl.when(jnp.logical_and(is_last, jnp.logical_and(keeps(c), me != c)))
            def _():
                out_copy(m, c).wait_send()

            return carry

        lax.fori_loop(0, segs, drain, 0)
        pltpu.make_async_copy(out.at[m], out.at[m], o_recv.at[m]).wait()
        return carry

    lax.fori_loop(0, batches, finish, 0)


def solution(mesh):
    segs = mesh.shape["segment"]

    def on_device(src, tgt, src_len, tgt_len, w_in, w_out, gains, final_gain):
        batches, seq, cw = src.shape
        group = segs // LAYERS
        w_in, w_out = w_in[0], w_out[0]
        width, qkv_cols = w_in.shape
        hc = w_out.shape[0]
        vmem = pl.BlockSpec(memory_space=pltpu.VMEM)
        smem = pl.BlockSpec(memory_space=pltpu.SMEM)
        anym = pl.BlockSpec(memory_space=pl.ANY)
        bf16 = jnp.bfloat16
        block = (segs, seq, cw)
        dma = pltpu.SemaphoreType.DMA
        return pl.pallas_call(
            functools.partial(kernel, segs),
            out_shape=jax.ShapeDtypeStruct(src.shape, src.dtype),
            in_specs=[smem, smem, vmem, vmem, anym, anym, vmem, vmem],
            out_specs=vmem,
            scratch_shapes=[
                pltpu.VMEM((width, qkv_cols), bf16),
                pltpu.VMEM((hc, width), bf16),
                pltpu.VMEM((2, batches) + block, bf16),
                pltpu.VMEM((2, seq, width), bf16),
                pltpu.VMEM((seq, qkv_cols), bf16),
                pltpu.VMEM((seq, hc), bf16),
                pltpu.VMEM(block, jnp.float32),
                pltpu.VMEM((batches,) + block, bf16),
                pltpu.VMEM((batches, group - 1) + block, bf16),
                pltpu.VMEM((batches,) + block, bf16),
                dma((2,)),
                dma((2, batches, segs)),
                dma((2, batches, group)),
                dma((batches, group - 1, segs)),
                dma((batches, group - 1, segs)),
                dma((batches, segs)),
                dma((batches,)),
            ],
            compiler_params=pltpu.CompilerParams(
                collective_id=0,
                has_side_effects=True,
                vmem_limit_bytes=56 * 1024 * 1024,
            ),
        )(src_len, tgt_len, src, tgt, w_in, w_out, gains, final_gain[None])

    return jax.shard_map(
        on_device,
        mesh=mesh,
        in_specs=(
            P("dp", None, "segment"),
            P("dp", None, "segment"),
            P("dp"),
            P("dp"),
            P("segment", None, None),
            P("segment", None, None),
            P(),
            P(),
        ),
        out_specs=P("dp", None, "segment"),
        check_vma=False,
    )
```

time: 424 us -> 158 us (0.37)
  waiting for transfers between devices: 247 us -> 0 us
  Pallas kernels: 0 us -> 156 us
  starting transfers between devices: 75.5 us -> 0 us
  matrix products: 47.3 us -> 0 us
  local copies, waits for them, and re-layouts: 29.2 us -> 1.67 us
  other arithmetic: 16.9 us -> 0 us
  loops' own time: 6.02 us -> 0 us
    ppermute x17 -> x0, waiting for transfers between devices: 199 us -> none  [the longest x7 121 us: partner(): return lax.ppermute(value, axis, pairs)]
    pallas_call x0 -> x1, Pallas kernels: none -> 156 us  [on_device(): pl.pallas_call(functools.partial(kernel, segs), out_shape=jax.ShapeDtypeS...]
    ppermute x17 -> x0, starting transfers between devices: 68.3 us -> none  [the longest x10 60.5 us: shifted(): return lax.ppermute(value, axis, pairs)]
    all_to_all x1 -> x0, waiting for transfers between devices: 48.2 us -> none  [on_device(): lax.all_to_all(outgoing, 'segment', split_axis=2, concat_axis=2, tiled=True)]
    dot_general x20 -> x0, matrix products: 45.3 us -> none  [the longest x4 18.8 us: head_partial(): jnp.dot(source, in_weight[:, head_cols:], preferred_element_type=jnp.floa...]
    dynamic_slice x31 -> x0, local copies, waits for them, and re-layouts: 22.6 us -> none  [the longest x30 21.5 us: pick_row(): return lax.dynamic_index_in_dim(array, row_slot, 0, keepdims=False)]
    dynamic_update_slice x7 -> x0, other arithmetic: 7.75 us -> none  [place_row(): lax.dynamic_update_index_in_dim(array, jnp.where(keep_flag, update, forme...]
    all_to_all x1 -> x0, starting transfers between devices: 7.28 us -> none  [on_device(): lax.all_to_all(outgoing, 'segment', split_axis=2, concat_axis=2, tiled=True)]
  transfers between devices with their start and end apart: 18 -> 0, of which waited for: 17 -> 0; matrix products, arithmetic and copies ran while one was open for 2% -> 0% of each run, Pallas kernels for 0% -> 0%
where the time goes in v1:
time: 158 us
  Pallas kernels  156 us (99%)
  local copies, waits for them, and re-layouts  1.67 us (1%)
    pallas_call x1, Pallas kernels, on_device(): pl.pallas_call(functools.partial(kernel, segs), out_shape=jax.ShapeDtypeS...  156 us

profile of v1, /device:TPU:0, one launch (start us, length us, event | category | flops | bytes accessed | tf_op | source)
XLA Modules:
  0.0 158.0 jit_solution(10665788896922677150)
XLA Ops:
  0.0 156.3 %shard_map.82 = bf16[4,128,256]{2,1,0:T(8,128)(2,1)} custom-call(s32[4]{0:T(128)} %src_len.1, s32[4]{0:T(128)} %tgt_len.1, bf16[4,128,256]{2,1,0:T(8,128)(2,1)} %src.1, bf16[4,128,256]{2,1,0:T(8,128)(2,1)} %tgt.1, bf16[2048,3072]{1,0:T(8,128)(2,1)} %bitcast.3, bf16[1024,2048]{1,0:T(8,128)(2,1)} %bitcast.4, f32[4,2048]{1,0:T(4,128)} %gains.1, f32[1,2048]{1,0:T(1,128)} %bitcast.5), custom_call_target="tpu_custom_call" | custom-call | tf_op jit(solution)/shard_map/pallas_call | solution.py:324
  156.3 1.7 %copy.10 = bf16[4,128,256]{2,1,0:T(8,128)(2,1)} copy(bf16[4,128,256]{2,1,0:T(8,128)(2,1)} %shard_map.82) | data formatting | bytes 524288

commit v2 on v1

--- a/solution.py
+++ b/solution.py
@@ -42,6 +42,12 @@
     p_recv,
     f_send,
     o_recv,
+    go,
+    side,
+    side_send,
+    side_recv,
+    on_send,
+    r_send,
 ):
     group = segs // LAYERS
     batches, seq, cw = src.shape
@@ -90,12 +96,17 @@
             target,
         )
 
+    def sends(kind, m, j):
+        if kind == 1:
+            return jnp.bool_(True)
+        return jnp.logical_or(j == member, jnp.logical_and(section == 0, m > 0))
+
     def send_inputs(kind, m):
         ref = src if kind == 0 else tgt
         for j in range(group):
             target = 2 * kind * group + j
 
-            @pl.when(me != target)
+            @pl.when(jnp.logical_and(sends(kind, m, j), me != target))
             def _():
                 input_copy(kind, m, j).start()
 
@@ -105,15 +116,89 @@
                     ref.at[m], act.at[kind, m, me], act_sem.at[kind, m, me]
                 ).start()
 
-    for m in range(batches):
-        send_inputs(0, m)
-    for m in range(batches):
-        send_inputs(1, m)
+    def beside(g):
+        return section * group + lax.rem(member + g, group)
+
+    def side_copy(m, g):
+        return remote(
+            src.at[m],
+            side.at[m - 1, g - 1],
+            side_send.at[m - 1, g - 1],
+            side_recv.at[m - 1, g - 1],
+            beside(g),
+        )
+
+    def side_on(m, g):
+        source = beside(group - g)
+        return remote(
+            side.at[m - 1, g - 1],
+            act.at[0, m, source],
+            on_send.at[m - 1, g - 1],
+            act_sem.at[0, m, source],
+            member,
+        )
+
+    def relay(c, g):
+        return remote(
+            act.at[0, 0, c],
+            act.at[0, 0, c],
+            r_send.at[g - 1, c],
+            act_sem.at[0, 0, c],
+            beside(g),
+        )
+
+    send_inputs(0, 0)
+
+    @pl.when(section > 0)
+    def _():
+        for m in range(1, batches):
+            for g in range(1, group):
+                side_copy(m, g).start()
+
+    @pl.when(section <= 2)
+    def _():
+        for m in range(batches):
+            send_inputs(1, m)
 
     def act_wait(kind, m, c):
         pltpu.make_async_copy(
             act.at[kind, m, c], act.at[kind, m, c], act_sem.at[kind, m, c]
         ).wait()
+
+    def pass_on():
+        for c in range(segs):
+
+            @pl.when(c % group == member)
+            def _(c=c):
+                act_wait(0, 0, c)
+                for g in range(1, group):
+                    relay(c, g).start()
+
+    @pl.when(section == 0)
+    def _():
+        pass_on()
+        for step in range(1, segs):
+            pl.semaphore_signal(
+                go,
+                inc=1,
+                device_id={"segment": lax.rem(me + step, segs)},
+                device_id_type=MESH,
+            )
+
+    pl.semaphore_wait(go, jnp.where(section == 0, group - 1, group))
+    for m in range(1, batches):
+        send_inputs(0, m)
+
+        @pl.when(section > 0)
+        def _(m=m):
+            for g in range(1, group):
+                side_copy(m, g).wait_recv()
+                side_on(m, g).start()
+
+    @pl.when(section > 2)
+    def _():
+        for m in range(batches):
+            send_inputs(1, m)
 
     def normalize(kind, m, gain_row):
         total = jnp.zeros((seq, cw), jnp.float32)
@@ -147,12 +232,15 @@
             target,
         )
 
-    def part_needed(c, g):
+    def whole(m):
+        return jnp.logical_and(section < LAYERS - 1, m > 0)
+
+    def part_needed(m, c, g):
         goal = lax.rem(member + g, group)
-        return jnp.logical_or(section < LAYERS - 1, lax.rem(c, group) == goal)
-
-    def keeps(c):
-        return jnp.logical_or(section < LAYERS - 1, lax.rem(c, group) == member)
+        return jnp.logical_or(whole(m), lax.rem(c, group) == goal)
+
+    def keeps(m, c):
+        return jnp.logical_or(whole(m), lax.rem(c, group) == member)
 
     def next_copy(m, c):
         return remote(
@@ -166,15 +254,22 @@
     kv_tiles = 2 * hc // tile
     q_tiles = hc // tile
 
-    def batch_step(m, carry):
+    def prepare(m):
         @pl.when(is_cross)
         def _():
             for c in range(segs):
                 act_wait(1, m, c)
             normalize(1, m, query_gain)
 
+        @pl.when(jnp.logical_and(section > 0, m == 0))
+        def _():
+            pass_on()
+
         for c in range(segs):
-            act_wait(0, m, c)
+
+            @pl.when(jnp.logical_or(m > 0, c % group != member))
+            def _(c=c):
+                act_wait(0, m, c)
 
         normalize(0, m, key_gain)
 
@@ -182,16 +277,16 @@
         def _():
             win_copy.wait()
 
-        def project(t, carry):
-            kind = jnp.where(t < q_tiles, q_src, 0)
-            cols = pl.ds(pl.multiple_of(t * tile, tile), tile)
-            qkv[:, cols] = jnp.dot(
-                nrm[kind], win[:, cols], preferred_element_type=jnp.float32
-            ).astype(jnp.bfloat16)
-            return carry
-
-        lax.fori_loop(0, q_tiles + kv_tiles, project, 0)
-
+
+    def project(t, carry):
+        kind = jnp.where(t < q_tiles, q_src, 0)
+        cols = pl.ds(pl.multiple_of(t * tile, tile), tile)
+        qkv[:, cols] = jnp.dot(
+            nrm[kind], win[:, cols], preferred_element_type=jnp.float32
+        ).astype(jnp.bfloat16)
+        return carry
+
+    def attend(m):
         length = jnp.where(is_last, tgt_len[m], src_len[m])
         keys = lax.broadcasted_iota(jnp.int32, (2 * seq, seq), 1)
         rows = lax.broadcasted_iota(jnp.int32, (2 * seq, seq), 0)
@@ -227,6 +322,7 @@
                 jnp.bfloat16
             )
 
+    def send_parts(m):
         @pl.when(m == 0)
         def _():
             wout_copy.wait()
@@ -238,7 +334,7 @@
             ps[m, c] = part.astype(jnp.bfloat16)
             for g in range(1, group):
 
-                @pl.when(part_needed(c, g))
+                @pl.when(part_needed(m, c, g))
                 def _():
                     part_copy(m, c, g).start()
 
@@ -246,54 +342,89 @@
 
         lax.fori_loop(0, segs, emit, 0)
 
-        def combine(c, carry):
-            @pl.when(keeps(c))
-            def _():
-                total = own[c] + act[q_src, m, c].astype(jnp.float32)
-                for g in range(1, group):
-                    part_copy(m, c, g).wait_recv()
-                    total = total + pr[m, g - 1, c].astype(jnp.float32)
-                fw[m, c] = total.astype(jnp.bfloat16)
-
-                @pl.when(section < LAYERS - 1)
-                def _():
-                    next_copy(m, c).start()
-
-                @pl.when(jnp.logical_and(is_last, me != c))
-                def _():
-                    out_copy(m, c).start()
-
-                @pl.when(jnp.logical_and(is_last, me == c))
-                def _():
-                    pltpu.make_async_copy(fw.at[m, c], out.at[m], o_recv.at[m]).start()
-
-            return carry
-
-        lax.fori_loop(0, segs, combine, 0)
+    def combine(m, c):
+        @pl.when(keeps(m, c))
+        def _():
+            total = own[c] + act[q_src, m, c].astype(jnp.float32)
+            for g in range(1, group):
+                part_copy(m, c, g).wait_recv()
+                total = total + pr[m, g - 1, c].astype(jnp.float32)
+            fw[m, c] = total.astype(jnp.bfloat16)
+
+            @pl.when(section < LAYERS - 1)
+            def _():
+                next_copy(m, c).start()
+
+            @pl.when(jnp.logical_and(is_last, me != c))
+            def _():
+                out_copy(m, c).start()
+
+            @pl.when(jnp.logical_and(is_last, me == c))
+            def _():
+                pltpu.make_async_copy(fw.at[m, c], out.at[m], o_recv.at[m]).start()
+
+    half = (q_tiles + kv_tiles) // 2
+    stages = (
+        prepare,
+        lambda m: lax.fori_loop(0, half, project, 0),
+        lambda m: lax.fori_loop(half, q_tiles + kv_tiles, project, 0),
+        attend,
+    )
+
+    def batch_step(t, carry):
+        m = t - 1
+
+        @pl.when(t > 0)
+        def _():
+            send_parts(m)
+
+        for c in range(segs):
+            for i, stage in enumerate(stages):
+                if c == segs // 2 + i * segs // 8:
+
+                    @pl.when(t < batches)
+                    def _(stage=stage):
+                        stage(t)
+
+            @pl.when(t > 0)
+            def _(c=c):
+                combine(m, c)
+
         return carry
 
-    lax.fori_loop(0, batches, batch_step, 0)
+    lax.fori_loop(0, batches + 1, batch_step, 0)
 
     def finish(m, carry):
         for kind in range(2):
             for j in range(group):
 
-                @pl.when(me != 2 * kind * group + j)
+                @pl.when(jnp.logical_and(sends(kind, m, j), me != 2 * kind * group + j))
                 def _():
                     input_copy(kind, m, j).wait_send()
 
+        @pl.when(jnp.logical_and(section > 0, m > 0))
+        def _():
+            for g in range(1, group):
+                side_copy(m, g).wait_send()
+                side_on(m, g).wait_send()
+
         def drain(c, carry):
             for g in range(1, group):
 
-                @pl.when(part_needed(c, g))
+                @pl.when(part_needed(m, c, g))
                 def _():
                     part_copy(m, c, g).wait_send()
 
-            @pl.when(section < LAYERS - 1)
+            @pl.when(jnp.logical_and(section < LAYERS - 1, keeps(m, c)))
             def _():
                 next_copy(m, c).wait_send()
 
-            @pl.when(jnp.logical_and(is_last, jnp.logical_and(keeps(c), me != c)))
+            @pl.when(jnp.logical_and(m == 0, lax.rem(c, group) == member))
+            def _():
+                for g in range(1, group):
+                    relay(c, g).wait_send()
+
+            @pl.when(jnp.logical_and(is_last, jnp.logical_and(keeps(m, c), me != c)))
             def _():
                 out_copy(m, c).wait_send()
 
@@ -344,6 +475,12 @@
                 dma((batches, group - 1, segs)),
                 dma((batches, segs)),
                 dma((batches,)),
+                pltpu.SemaphoreType.REGULAR,
+                pltpu.VMEM((batches - 1, group - 1, seq, cw), bf16),
+                dma((batches - 1, group - 1)),
+                dma((batches - 1, group - 1)),
+                dma((batches - 1, group - 1)),
+                dma((group - 1, segs)),
             ],
             compiler_params=pltpu.CompilerParams(
                 collective_id=0,

time: 158 us -> 135 us (0.85)
  Pallas kernels: 156 us -> 133 us
    pallas_call x1, Pallas kernels: 156 us -> 133 us  [on_device(): pl.pallas_call(functools.partial(kernel, segs), out_shape=jax.ShapeDtypeS...]
where the time goes in v2:
time: 135 us
  Pallas kernels  133 us (99%)
  local copies, waits for them, and re-layouts  1.67 us (1%)
    pallas_call x1, Pallas kernels, on_device(): pl.pallas_call(functools.partial(kernel, segs), out_shape=jax.ShapeDtypeS...  133 us

profile of v2, /device:TPU:0, one launch (start us, length us, event | category | flops | bytes accessed | tf_op | source)
XLA Modules:
  0.0 135.2 jit_solution(11953789605297925777)
XLA Ops:
  0.0 133.5 %shard_map.82 = bf16[4,128,256]{2,1,0:T(8,128)(2,1)} custom-call(s32[4]{0:T(128)} %src_len.1, s32[4]{0:T(128)} %tgt_len.1, bf16[4,128,256]{2,1,0:T(8,128)(2,1)} %src.1, bf16[4,128,256]{2,1,0:T(8,128)(2,1)} %tgt.1, bf16[2048,3072]{1,0:T(8,128)(2,1)} %bitcast.3, bf16[1024,2048]{1,0:T(8,128)(2,1)} %bitcast.4, f32[4,2048]{1,0:T(4,128)} %gains.1, f32[1,2048]{1,0:T(1,128)} %bitcast.5), custom_call_target="tpu_custom_call" | custom-call | tf_op jit(solution)/shard_map/pallas_call | solution.py:455
  133.5 1.7 %copy.10 = bf16[4,128,256]{2,1,0:T(8,128)(2,1)} copy(bf16[4,128,256]{2,1,0:T(8,128)(2,1)} %shard_map.82) | data formatting | bytes 524288

commit v3 on v2

--- a/solution.py
+++ b/solution.py
@@ -340,7 +340,7 @@
 
             return carry
 
-        lax.fori_loop(0, segs, emit, 0)
+        lax.fori_loop(0, segs, emit, 0, unroll=True)
 
     def combine(m, c):
         @pl.when(keeps(m, c))
@@ -366,8 +366,8 @@
     half = (q_tiles + kv_tiles) // 2
     stages = (
         prepare,
-        lambda m: lax.fori_loop(0, half, project, 0),
-        lambda m: lax.fori_loop(half, q_tiles + kv_tiles, project, 0),
+        lambda m: lax.fori_loop(0, half, project, 0, unroll=True),
+        lambda m: lax.fori_loop(half, q_tiles + kv_tiles, project, 0, unroll=True),
         attend,
     )
 

time: 135 us -> 131 us (0.970)
  Pallas kernels: 133 us -> 129 us
    pallas_call x1, Pallas kernels: 133 us -> 129 us  [on_device(): pl.pallas_call(functools.partial(kernel, segs), out_shape=jax.ShapeDtypeS...]
where the time goes in v3:
time: 131 us
  Pallas kernels  129 us (98%)
  local copies, waits for them, and re-layouts  1.67 us (1%)
    pallas_call x1, Pallas kernels, on_device(): pl.pallas_call(functools.partial(kernel, segs), out_shape=jax.ShapeDtypeS...  129 us

profile of v3, /device:TPU:0, one launch (start us, length us, event | category | flops | bytes accessed | tf_op | source)
XLA Modules:
  0.0 131.0 jit_solution(11911070578014598525)
XLA Ops:
  0.0 129.4 %shard_map.82 = bf16[4,128,256]{2,1,0:T(8,128)(2,1)} custom-call(s32[4]{0:T(128)} %src_len.1, s32[4]{0:T(128)} %tgt_len.1, bf16[4,128,256]{2,1,0:T(8,128)(2,1)} %src.1, bf16[4,128,256]{2,1,0:T(8,128)(2,1)} %tgt.1, bf16[2048,3072]{1,0:T(8,128)(2,1)} %bitcast.3, bf16[1024,2048]{1,0:T(8,128)(2,1)} %bitcast.4, f32[4,2048]{1,0:T(4,128)} %gains.1, f32[1,2048]{1,0:T(1,128)} %bitcast.5), custom_call_target="tpu_custom_call" | custom-call | tf_op jit(solution)/shard_map/pallas_call | solution.py:455
  129.4 1.7 %copy.10 = bf16[4,128,256]{2,1,0:T(8,128)(2,1)} copy(bf16[4,128,256]{2,1,0:T(8,128)(2,1)} %shard_map.82) | data formatting | bytes 524288
